TPU v7x, 32 devices: a whole 2x2x4 slice. The times are simulated.
32 devices in a mesh: dp: 16 (over z, x, core), tensor: 2 (over y).
Axes of the slice: x: 2, y: 2, z: 4, core: 2. Of those that a mesh axis runs over, the one named last changes fastest.
Arguments:
- hidden: bfloat16 [5120, 18432], P('dp', 'tensor'), may hold values from -6 to 6
- fixed_down_weight: bfloat16 [18432, 4608], P('tensor', 'dp'), may hold values from -4 to 4
- lowrank_factor_b: bfloat16 [18432, 16], P('tensor'), may hold values from -0.046875 to 0.046875
- lowrank_factor_a: bfloat16 [16, 4608], P(None, 'dp'), may hold values from -1.5 to 1.5
- magnitude: float32 [4608], P('tensor'), may hold values from 0.5 to 2
- cotangent: bfloat16 [5120, 4608], P('dp', 'tensor'), may hold values from -0.083496094 to 0.083496094
Outputs:
- mixed: bfloat16 [5120, 4608], P('dp', 'tensor')
- gradient_column_scale: float32 [4608], P(('tensor', 'dp'))
- gradient_factor_a: float32 [16, 4608], P(None, ('tensor', 'dp'))
- gradient_factor_b: float32 [18432, 16], P(('tensor', 'dp'))
All inputs are finite; a program needn't handle non-finite values.
Results may differ from a plain program's by a relative error of at most 0.0054.
Values may be sent and summed in bfloat16 or wider, within the bound.
A program may use at most 192 MiB of HBM per device.

v0:
```python
import jax
import jax.numpy as jnp
from jax import lax
from jax.sharding import Mesh, PartitionSpec as P

F32, BF16 = (jnp.float32, jnp.bfloat16)


def body(hidden, weight, factor_b, factor_a, magnitude, cotangent, *, n_out, n_in, n_t):
    rows, depth = hidden.shape
    cols = weight.shape[1]
    rank = factor_b.shape[1]
    out_cols = magnitude.shape[0]
    group = 2 * n_in
    dp = ("outer", "mid", "core")
    outer = lax.axis_index("outer")
    place = lax.axis_index("mid") * 2 + lax.axis_index("core")
    own = lax.axis_index("tensor")
    swap_mid = [(i, (i + 1) % n_in) for i in range(n_in)]
    swap_core = [(0, 1), (1, 0)]
    h_mid = lax.ppermute(hidden, "mid", swap_mid)
    w_all = lax.all_gather(weight, "outer", axis=1, tiled=True)
    h_core = lax.ppermute(hidden, "core", swap_core)
    h_both = lax.ppermute(h_mid, "core", swap_core)
    low_part = jnp.dot(hidden, factor_b, preferred_element_type=F32)
    merged = weight.astype(F32) + jnp.dot(factor_b, factor_a, preferred_element_type=F32)
    local_sq = jnp.sum(merged * merged, axis=0)
    low, block_sq = lax.psum((low_part, local_sq), "tensor")
    col_sq = lax.all_gather(block_sq, dp, axis=0, tiled=True)
    full_a = lax.all_gather(factor_a, dp, axis=1, tiled=True)
    norms = jnp.sqrt(lax.dynamic_slice_in_dim(col_sq, own * out_cols, out_cols, 0) + 1e-06)
    scale = magnitude / norms
    low_b = low.astype(BF16)
    own_a = lax.dynamic_slice_in_dim(full_a, own * out_cols, out_cols, 1)
    adapter = jnp.dot(low_b, own_a, preferred_element_type=F32)
    h_all = jnp.zeros((group, rows, depth), BF16)
    for block, flip in ((hidden, 0), (h_core, 1), (h_mid, 2), (h_both, 3)):
        h_all = lax.dynamic_update_slice_in_dim(h_all, block[None], place ^ flip, 0)
    h_rows = h_all.reshape(group * rows, depth)
    cot = cotangent.astype(F32)
    dpre_b = (cot * scale).astype(BF16)
    back_b = lax.psum(jnp.dot(dpre_b, own_a.T, preferred_element_type=F32), "tensor").astype(BF16)
    b_part = jnp.dot(back_b.T, hidden, preferred_element_type=F32)
    a_part = jnp.dot(low_b.T, dpre_b, preferred_element_type=F32)
    n_dp = n_out * group
    parts = jnp.concatenate([x.reshape(rank, n_dp, -1) for x in (a_part, b_part)], axis=2)
    parts = lax.all_to_all(parts.transpose(1, 0, 2), dp, 0, 0, tiled=True)
    sums = jnp.sum(parts, axis=0)
    grad_a = sums[:, : out_cols // n_dp]
    grad_b = sums[:, out_cols // n_dp :].T
    w_all, grad_a, grad_b = lax.optimization_barrier((w_all, grad_a, grad_b))
    per_t = n_out // n_t
    sends = jnp.dot(h_rows, w_all, preferred_element_type=F32).astype(BF16)
    sends = sends.reshape(group, rows, n_t, per_t, cols).transpose(2, 0, 3, 1, 4)
    sends = sends.reshape(n_t * group, per_t, rows, cols)
    got = lax.all_to_all(sends, ("tensor", "mid", "core"), 0, 0, tiled=True)
    got = got.reshape(n_t, group, per_t, rows, cols)
    summed = jnp.sum(got.astype(F32), axis=0).transpose(2, 1, 0, 3).reshape(rows, out_cols)
    pre = summed + adapter
    mixed = (pre * scale).astype(BF16)
    mag_part = jnp.sum(cot * pre, axis=0) / norms
    for axis in ("core", "mid", "outer"):
        mag_part = lax.psum(mag_part, axis)
    at = (outer * group + place) * (out_cols // n_dp)
    grad_scale = lax.dynamic_slice_in_dim(mag_part, at, out_cols // n_dp, 0)
    return (mixed, grad_scale, grad_a, grad_b)


def solution(mesh):
    n_dp, n_t = (mesh.shape["dp"], mesh.shape["tensor"])
    n_in = 2
    n_out = n_dp // (2 * n_in)
    fine = Mesh(mesh.devices.reshape(n_out, n_in, 2, n_t), ("outer", "mid", "core", "tensor"))
    dp = ("outer", "mid", "core")

    def step(*args):
        return body(*args, n_out=n_out, n_in=n_in, n_t=n_t)

    return jax.shard_map(
        step,
        mesh=fine,
        in_specs=(
            P(dp, "tensor"),
            P("tensor", dp),
            P("tensor", None),
            P(None, dp),
            P("tensor"),
            P(dp, "tensor"),
        ),
        out_specs=(
            P(dp, "tensor"),
            P(("tensor",) + dp),
            P(None, ("tensor",) + dp),
            P(("tensor",) + dp, None),
        ),
        check_vma=False,
    )
```

profile of v0, /device:TPU:0, one launch (start us, length us, event | category | flops | bytes accessed | tf_op | source)
XLA Modules:
  0.0 534.6 jit_solution(16286039173848104964)
XLA Ops:
  7.2 0.7 all-gather.3.cloned.1.call-update
  7.9 3.0 collective-permute-start.1
  11.0 144.5 %all-gather = bf16[16,288,16]{1,2,0:T(8,128)(2,1)S(1)} all-gather(bf16[1,288,16]{1,2,0:T(8,128)(2,1)} %bitcast.44), channel_id=1, replica_groups=mesh['outer'=4,'mid'=2,'core'=2,'tensor'=2] {'outer','mid','core'}, dimensions={0}, use_global_device_ids=true | all-gather | bytes 156672 | tf_op jit(solution)/shard_map/all_gather | solution.py:30
  157.0 4.4 fusion.3
  161.4 4.9 psum.43
  166.5 80.5 %all-reduce = f32[4608]{0:T(1024)S(1)} all-reduce(f32[4608]{0:T(1024)S(1)} %dynamic-update-slice), channel_id=1, replica_groups=mesh['outer'=4,'mid'=2,'core'=2,'tensor'=2] {'outer','mid','core'}, use_global_device_ids=true, to_apply=%add | all-reduce | flops 4608 | bytes 36864
  247.7 4.4 fusion.18
  252.1 8.6 %all-reduce.1 = (bf16[320,16]{0,1:T(8,128)(2,1)S(1)}, bf16[320,16]{0,1:T(8,128)(2,1)S(1)}) all-reduce(f32[320,16]{0,1:T(8,128)S(1)} %fusion.4, f32[320,16]{0,1:T(8,128)S(1)} %fusion.18), channel_id=1, replica_groups=mesh['outer'=4,'mid'=2,'core'=2,'tensor'=2] {'tensor'}, use_global_device_ids=true, to_apply=%region_3.0 | all-reduce | flops 10240 | bytes 61440 | tf_op jit(solution)/shard_map/psum | solution.py:42
  261.4 3.7 fusion.19
  265.6 1.1 maximum_bitcast_fusion
  266.7 16.8 %all-to-all-start = ((f32[16,16,720]{2,1,0:T(8,128)}), f32[16,16,720]{2,1,0:T(8,128)S(1)}, u32[]{:S(2)}, u32[]{:S(2)}) async-start(f32[16,16,720]{2,1,0:T(8,128)} %maximum_bitcast_fusion), calls=%async_computation | async-start | bytes 1572864 | tf_op jit(solution)/shard_map/all_to_all | solution.py:47
  284.0 8.7 %broadcast_in_dim.17 = bf16[4,320,9216]{2,1,0:T(8,128)(2,1)} broadcast(bf16[]{:T(256)} %constant.14.clone.1), dimensions={} | broadcast | bytes 23592962 | tf_op jit(solution)/shard_map/broadcast_in_dim | solution.py:36
  292.7 2.9 bitcast_dynamic-update-slice_fusion.3
  295.6 25.9 %all-to-all-done = f32[16,16,720]{2,1,0:T(8,128)S(1)} async-done(((f32[16,16,720]{2,1,0:T(8,128)}), f32[16,16,720]{2,1,0:T(8,128)S(1)}, u32[]{:S(2)}, u32[]{:S(2)}) %all-to-all-start) | async-done | bytes 737312 | tf_op jit(solution)/shard_map/all_to_all | solution.py:47
  322.2 0.7 slice_bitcast_fusion
  322.9 5.6 %bitcast_dynamic-update-slice_fusion.2 = bf16[4,320,9216]{2,1,0:T(8,128)(2,1)} fusion(bf16[4,320,9216]{2,1,0:T(8,128)(2,1)} %bitcast_dynamic-update-slice_fusion.3, s32[]{:T(128)S(6)} %select_n.20, bf16[320,9216]{1,0:T(8,128)(2,1)} %collective-permute-done), kind=kLoop, calls=%fused_computation.6 | loop fusion | bytes 11796484 | tf_op jit(solution)/shard_map/dynamic_update_slice | solution.py:38
  328.5 5.6 %bitcast_dynamic-update-slice_fusion.1 = bf16[4,320,9216]{2,1,0:T(8,128)(2,1)} fusion(bf16[4,320,9216]{2,1,0:T(8,128)(2,1)} %bitcast_dynamic-update-slice_fusion.2, s32[]{:T(128)S(6)} %select_n.21, bf16[320,9216]{1,0:T(8,128)(2,1)} %collective-permute-done.1), kind=kLoop, calls=%fused_computation.5 | loop fusion | bytes 11796484 | tf_op jit(solution)/shard_map/dynamic_update_slice | solution.py:38
  334.1 5.6 %bitcast_dynamic-update-slice_fusion = bf16[4,320,9216]{2,1,0:T(8,128)(2,1)} fusion(bf16[4,320,9216]{2,1,0:T(8,128)(2,1)} %bitcast_dynamic-update-slice_fusion.1, s32[]{:T(128)S(6)} %select_n.22, bf16[320,9216]{1,0:T(8,128)(2,1)} %collective-permute-done.2), kind=kLoop, calls=%fused_computation.4 | loop fusion | bytes 11796484 | tf_op jit(solution)/shard_map/dynamic_update_slice | solution.py:38
  339.6 51.8 %all-gather.3.cloned.1.call-done = bf16[9216,1152]{0,1:T(8,128)(2,1)} async-done(((bf16[9216,288]{0,1:T(8,128)(2,1)}), bf16[9216,1152]{0,1:T(8,128)(2,1)}) %all-gather.3.cloned.1.call-update) | async-done | bytes 21233680 | tf_op jit(solution)/shard_map/all_gather | solution.py:22
  391.4 37.6 %convolution_convert_fusion = bf16[1280,1152]{1,0:T(8,128)(2,1)} fusion(bf16[1280,9216]{1,0:T(8,128)(2,1)} %bitcast.39, bf16[9216,1152]{0,1:T(8,128)(2,1)} %all-gather.3.cloned.1.call-done), kind=kOutput, calls=%fused_computation.2 | convolution fusion | flops 27180564480 | bytes 47775744 | tf_op jit(solution)/shard_map/dot_general | solution.py:53
  429.0 3.9 copy.17
  433.0 5.1 reshape.33
  438.1 4.3 copy.18
  442.4 4.5 all-to-all-start.1
  446.9 42.1 %all-to-all-done.1 = bf16[8,2,320,288]{2,3,1,0:T(8,128)(2,1)} async-done(((bf16[8,2,320,288]{2,3,1,0:T(8,128)(2,1)}), bf16[8,2,320,288]{2,3,1,0:T(8,128)(2,1)}, u32[]{:S(2)}, u32[]{:S(2)}) %all-to-all-start.1) | async-done | bytes 2949152 | tf_op jit(solution)/shard_map/all_to_all | solution.py:56
  488.9 3.1 convert_reduce_fusion
  492.1 2.0 copy.19
  494.1 3.3 copy.20
  497.4 3.2 fusion.2
  500.7 3.3 psum.45
  504.0 7.1 %psum.46 = f32[2304]{0:T(1024)S(1)} all-reduce(f32[2304]{0:T(1024)S(1)} %psum.45), channel_id=1, replica_groups=mesh['outer'=4,'mid'=2,'core'=2,'tensor'=2] {'mid'}, use_global_device_ids=true, to_apply=%region_8.0 | all-reduce | flops 2304 | bytes 18432 | tf_op jit(solution)/shard_map/psum | solution.py:63
  511.1 16.0 %psum.47 = f32[2304]{0:T(1024)S(1)} all-reduce(f32[2304]{0:T(1024)S(1)} %psum.46), channel_id=1, replica_groups=mesh['outer'=4,'mid'=2,'core'=2,'tensor'=2] {'outer'}, use_global_device_ids=true, to_apply=%region_9.0 | all-reduce | flops 2304 | bytes 18432 | tf_op jit(solution)/shard_map/psum | solution.py:63
  (39 shorter events, 4.7 us)
Async XLA Ops:
  7.2 149.8 %copy-start = (bf16[9216,16]{0,1:T(8,128)(2,1)S(1)}, bf16[9216,16]{0,1:T(8,128)(2,1)}, u32[]{:S(2)}) copy-start(bf16[9216,16]{0,1:T(8,128)(2,1)} %param.8) | copy-start | bytes 884740
  7.2 148.6 %copy-start.5 = (u32[32]{0:T(128)S(1)}, u32[32]{0:T(128)}, u32[]{:S(2)}) copy-start(u32[32]{0:T(128)} %constant.38) | copy-start | bytes 388
  7.2 149.8 %copy-start.3 = (bf16[16,288]{1,0:T(8,128)(2,1)S(1)}, bf16[16,288]{1,0:T(8,128)(2,1)}, u32[]{:S(2)}) copy-start(bf16[16,288]{1,0:T(8,128)(2,1)} %param.9) | copy-start | bytes 27652
  7.2 384.2 %all-gather.3.cloned.1.call-start = ((), (), s32[]{:S(2)}) async-start(), calls=%async_computation.2 | async-start | bytes 26542080 | tf_op jit(solution)/shard_map/all_gather | solution.py:22
  7.9 275.6 %collective-permute-start.1 = (bf16[320,9216]{1,0:T(8,128)(2,1)}, bf16[320,9216]{1,0:T(8,128)(2,1)}, u32[]{:S(2)}, u32[]{:S(2)}) collective-permute-start(bf16[320,9216]{1,0:T(8,128)(2,1)} %param.6), channel_id=1, source_target_pairs={{0,4},{4,0},{1,5},{5,1},{2,6},{6,2},{3,7},{7,3},{8,12},{12,8},{9,1... | collective-permute-start | bytes 17694728 | tf_op jit(solution)/shard_map/ppermute | solution.py:21
  11.0 311.9 %collective-permute-start = (bf16[320,9216]{1,0:T(8,128)(2,1)}, bf16[320,9216]{1,0:T(8,128)(2,1)}, u32[]{:S(2)}, u32[]{:S(2)}) collective-permute-start(bf16[320,9216]{1,0:T(8,128)(2,1)} %param.6), channel_id=1, source_target_pairs={{0,2},{2,0},{1,3},{3,1},{4,6},{6,4},{5,7},{7,5},{8,10},{10,8},{9,1... | collective-permute-start | bytes 17694728 | tf_op jit(solution)/shard_map/ppermute | solution.py:23
  157.0 90.1 %copy-start.4 = (f32[2304]{0:T(1024)S(1)}, f32[2304]{0:T(1024)}, u32[]{:S(2)}) copy-start(f32[2304]{0:T(1024)} %param.10) | copy-start | bytes 27652
  157.0 90.2 %copy-start.2 = (bf16[320,2304]{1,0:T(8,128)(2,1)S(1)}, bf16[320,2304]{1,0:T(8,128)(2,1)}, u32[]{:S(2)}) copy-start(bf16[320,2304]{1,0:T(8,128)(2,1)} %param.11) | copy-start | bytes 4423684
  266.7 54.8 %all-to-all-start = ((f32[16,16,720]{2,1,0:T(8,128)}), f32[16,16,720]{2,1,0:T(8,128)S(1)}, u32[]{:S(2)}, u32[]{:S(2)}) async-start(f32[16,16,720]{2,1,0:T(8,128)} %maximum_bitcast_fusion), calls=%async_computation | async-start | bytes 1572864 | tf_op jit(solution)/shard_map/all_to_all | solution.py:47
  283.5 9.2 %slice-start = ((s8[5898240]{0:T(1024)(128)(4,1)}), s8[1703936]{0:T(1024)(128)(4,1)S(1)}, s32[]{:S(2)}) async-start(s8[5898240]{0:T(1024)(128)(4,1)} %bitcast.37), calls=%async_computation.3 | async-start | bytes 3407872
  283.5 9.2 %slice-start.1 = ((s8[5898240]{0:T(1024)(128)(4,1)}), s8[4194304]{0:T(1024)(128)(4,1)S(1)}, s32[]{:S(2)}) async-start(s8[5898240]{0:T(1024)(128)(4,1)} %bitcast.37), calls=%async_computation.4 | async-start | bytes 8388608
  283.5 50.5 %collective-permute-start.2 = (bf16[320,9216]{1,0:T(8,128)(2,1)}, bf16[320,9216]{1,0:T(8,128)(2,1)}, u32[]{:S(2)}, u32[]{:S(2)}) collective-permute-start(bf16[320,9216]{1,0:T(8,128)(2,1)} %collective-permute-done.1), channel_id=1, source_target_pairs={{0,2},{2,0},{1,3},{3,1},{4,6},{6,4},{5,7},{7,5},{8,10},{10,8},{9,1... | collective-permute-start | bytes 17694728 | tf_op jit(solution)/shard_map/ppermute | solution.py:24
  442.4 46.6 %all-to-all-start.1 = ((bf16[8,2,320,288]{2,3,1,0:T(8,128)(2,1)}), bf16[8,2,320,288]{2,3,1,0:T(8,128)(2,1)}, u32[]{:S(2)}, u32[]{:S(2)}) async-start(bf16[8,2,320,288]{2,3,1,0:T(8,128)(2,1)} %bitcast.40), calls=%async_computation.1 | async-start | bytes 7077888 | tf_op jit(solution)/shard_map/all_to_all | solution.py:56
  494.1 33.6 %copy-start.1 = (bf16[9216,16]{0,1:T(8,128)(2,1)S(1)}, bf16[9216,16]{0,1:T(8,128)(2,1)}, u32[]{:S(2)}) copy-start(bf16[9216,16]{0,1:T(8,128)(2,1)} %param.8) | copy-start | bytes 884740
Sparse Core Ops, SparseCore 0:
  9.6 381.7 all-gather.2
where the time goes:
time: 535 us
  blocking collectives  265 us (50%)
  waiting for transfers between devices  120 us (22%)
  matrix products  54.2 us (10%)
  local copies, waits for them, and re-layouts  50.8 us (9%)
  starting transfers between devices  24.8 us (5%)
  between operations  14.9 us (3%)
    all_gather x1, blocking collectives, body(): full_a = lax.all_gather(factor_a, dp, axis=1, tiled=True)  145 us
    unnamed x1, blocking collectives  80.5 us
    all_gather x1, waiting for transfers between devices, body(): w_all = lax.all_gather(weight, 'outer', axis=1, tiled=True)  51.8 us
    all_to_all x1, waiting for transfers between devices, body(): got = lax.all_to_all(sends, ('tensor', 'mid', 'core'), 0, 0, tiled=True)  42.1 us
    dot_general x1, matrix products, body(): sends = jnp.dot(h_rows, w_all, preferred_element_type=F32).astype(BF16)  37.6 us
    psum x3, blocking collectives, body(): mag_part = lax.psum(mag_part, axis)  26.4 us
    all_to_all x1, waiting for transfers between devices, body(): parts = lax.all_to_all(parts.transpose(1, 0, 2), dp, 0, 0, tiled=True)  25.9 us
    dynamic_update_slice x4, local copies, waits for them, and re-layouts, body(): h_all = lax.dynamic_update_slice_in_dim(h_all, block[None], place ^ flip, 0)  19.6 us
  transfers between devices with their start and end apart: 6, of which 3 were waited for; matrix products, arithmetic and copies ran while one was open for 9% of the time, Pallas kernels for 0%

commit v1 on v0

--- a/solution.py
+++ b/solution.py
@@ -19,7 +19,7 @@
     swap_mid = [(i, (i + 1) % n_in) for i in range(n_in)]
     swap_core = [(0, 1), (1, 0)]
     h_mid = lax.ppermute(hidden, "mid", swap_mid)
-    w_all = lax.all_gather(weight, "outer", axis=1, tiled=True)
+    w_all = jnp.concatenate(lax.all_gather(weight, "outer"), axis=1)
     h_core = lax.ppermute(hidden, "core", swap_core)
     h_both = lax.ppermute(h_mid, "core", swap_core)
     low_part = jnp.dot(hidden, factor_b, preferred_element_type=F32)

time: 535 us -> 587 us (1.097)
  local copies, waits for them, and re-layouts: 50.8 us -> 101 us
    all_gather x0 -> x1, local copies, waits for them, and re-layouts: none -> 33.4 us  [body(): w_all = jnp.concatenate(lax.all_gather(weight, 'outer'), axis=1)]
    reshape x0 -> x1, local copies, waits for them, and re-layouts: none -> 17.1 us  [body(): w_all = jnp.concatenate(lax.all_gather(weight, 'outer'), axis=1)]
  transfers between devices with their start and end apart: 6 -> 6, of which waited for: 3 -> 3; matrix products, arithmetic and copies ran while one was open for 9% -> 8% of each run, Pallas kernels for 0% -> 0%
where the time goes in v1:
time: 587 us; the launch traced here: 585 us
  blocking collectives  265 us (45%)
  waiting for transfers between devices  120 us (20%)
  local copies, waits for them, and re-layouts  101 us (17%)
  matrix products  54.2 us (9%)
  starting transfers between devices  25 us (4%)
  between operations  14.9 us (3%)
    all_gather x1, blocking collectives, body(): full_a = lax.all_gather(factor_a, dp, axis=1, tiled=True)  145 us
    unnamed x1, blocking collectives  80.5 us
    all_gather x1, waiting for transfers between devices, body(): w_all = jnp.concatenate(lax.all_gather(weight, 'outer'), axis=1)  51.8 us
    all_to_all x1, waiting for transfers between devices, body(): got = lax.all_to_all(sends, ('tensor', 'mid', 'core'), 0, 0, tiled=True)  41.8 us
    dot_general x1, matrix products, body(): sends = jnp.dot(h_rows, w_all, preferred_element_type=F32).astype(BF16)  37.6 us
    all_gather x1, local copies, waits for them, and re-layouts, body(): w_all = jnp.concatenate(lax.all_gather(weight, 'outer'), axis=1)  33.4 us
    psum x3, blocking collectives, body(): mag_part = lax.psum(mag_part, axis)  26.3 us
    all_to_all x1, waiting for transfers between devices, body(): parts = lax.all_to_all(parts.transpose(1, 0, 2), dp, 0, 0, tiled=True)  25.9 us
  transfers between devices with their start and end apart: 6, of which 3 were waited for; matrix products, arithmetic and copies ran while one was open for 8% of the time, Pallas kernels for 0%

profile of v1, /device:TPU:0, one launch (start us, length us, event | category | flops | bytes accessed | tf_op | source)
XLA Modules:
  0.0 584.9 jit_solution(12785664437475302987)
XLA Ops:
  7.9 3.0 collective-permute-start.1
  11.0 144.5 %all-gather.1 = bf16[16,288,16]{1,2,0:T(8,128)(2,1)S(1)} all-gather(bf16[1,288,16]{1,2,0:T(8,128)(2,1)} %bitcast.50), channel_id=1, replica_groups=mesh['outer'=4,'mid'=2,'core'=2,'tensor'=2] {'outer','mid','core'}, dimensions={0}, use_global_device_ids=true | all-gather | bytes 156672 | tf_op jit(solution)/shard_map/all_gather | solution.py:30
  157.0 4.4 fusion.3
  161.4 4.9 psum.43
  166.5 80.5 %all-reduce = f32[4608]{0:T(1024)S(1)} all-reduce(f32[4608]{0:T(1024)S(1)} %dynamic-update-slice), channel_id=1, replica_groups=mesh['outer'=4,'mid'=2,'core'=2,'tensor'=2] {'outer','mid','core'}, use_global_device_ids=true, to_apply=%add | all-reduce | flops 4608 | bytes 36864
  247.6 4.4 fusion.18
  252.0 8.6 %all-reduce.1 = (bf16[320,16]{0,1:T(8,128)(2,1)S(1)}, bf16[320,16]{0,1:T(8,128)(2,1)S(1)}) all-reduce(f32[320,16]{0,1:T(8,128)S(1)} %fusion.4, f32[320,16]{0,1:T(8,128)S(1)} %fusion.18), channel_id=1, replica_groups=mesh['outer'=4,'mid'=2,'core'=2,'tensor'=2] {'tensor'}, use_global_device_ids=true, to_apply=%region_3.0 | all-reduce | flops 10240 | bytes 61440 | tf_op jit(solution)/shard_map/psum | solution.py:42
  260.6 3.7 fusion.19
  265.5 1.1 maximum_bitcast_fusion
  266.6 16.8 %all-to-all-start = ((f32[16,16,720]{2,1,0:T(8,128)}), f32[16,16,720]{2,1,0:T(8,128)S(1)}, u32[]{:S(2)}, u32[]{:S(2)}) async-start(f32[16,16,720]{2,1,0:T(8,128)} %maximum_bitcast_fusion), calls=%async_computation | async-start | bytes 1572864 | tf_op jit(solution)/shard_map/all_to_all | solution.py:47
  283.9 8.7 %broadcast_in_dim.17 = bf16[4,320,9216]{2,1,0:T(8,128)(2,1)} broadcast(bf16[]{:T(256)} %constant.14.clone.1), dimensions={} | broadcast | bytes 23592962 | tf_op jit(solution)/shard_map/broadcast_in_dim | solution.py:36
  292.6 2.9 bitcast_dynamic-update-slice_fusion.3
  295.5 25.9 %all-to-all-done = f32[16,16,720]{2,1,0:T(8,128)S(1)} async-done(((f32[16,16,720]{2,1,0:T(8,128)}), f32[16,16,720]{2,1,0:T(8,128)S(1)}, u32[]{:S(2)}, u32[]{:S(2)}) %all-to-all-start) | async-done | bytes 737312 | tf_op jit(solution)/shard_map/all_to_all | solution.py:47
  322.8 5.6 bitcast_dynamic-update-slice_fusion.2
  328.4 5.6 bitcast_dynamic-update-slice_fusion.1
  334.0 5.6 bitcast_dynamic-update-slice_fusion
  339.6 51.8 %all-gather.4.cloned.1.call-done = bf16[36864,288]{0,1:T(8,128)(2,1)} async-done(((bf16[9216,288]{0,1:T(8,128)(2,1)}), bf16[36864,288]{0,1:T(8,128)(2,1)}) %all-gather.4.cloned.1.call-update) | async-done | bytes 21233680 | tf_op jit(solution)/shard_map/all_gather | solution.py:22
  391.4 33.4 %reshape.45 = bf16[4,9216,288]{1,0,2:T(4,128)(2,1)} reshape(bf16[36864,288]{0,1:T(8,128)(2,1)} %all-gather.4.cloned.1.call-done) | data formatting | bytes 42467328 | tf_op jit(solution)/shard_map/all_gather | solution.py:22
  424.7 17.1 %copy.19 = bf16[9216,4,288]{0,2,1:T(8,128)(2,1)} copy(bf16[9216,4,288]{0,1,2:T(4,128)(2,1)} %bitcast.43) | data formatting | bytes 42467328 | tf_op jit(solution)/shard_map/reshape | solution.py:22
  441.8 37.6 %convolution_convert_fusion = bf16[1280,1152]{1,0:T(8,128)(2,1)} fusion(bf16[1280,9216]{1,0:T(8,128)(2,1)} %bitcast.44, bf16[9216,1152]{0,1:T(8,128)(2,1)} %bitcast.45), kind=kOutput, calls=%fused_computation.2 | convolution fusion | flops 27180564480 | bytes 47775744 | tf_op jit(solution)/shard_map/dot_general | solution.py:53
  479.4 3.9 copy.23
  483.4 5.1 reshape.41
  488.5 4.3 copy.24
  492.8 4.7 all-to-all-start.1
  497.5 41.8 %all-to-all-done.1 = bf16[8,2,320,288]{2,3,1,0:T(8,128)(2,1)} async-done(((bf16[8,2,320,288]{2,3,1,0:T(8,128)(2,1)}), bf16[8,2,320,288]{2,3,1,0:T(8,128)(2,1)}, u32[]{:S(2)}, u32[]{:S(2)}) %all-to-all-start.1) | async-done | bytes 2949152 | tf_op jit(solution)/shard_map/all_to_all | solution.py:56
  539.3 3.1 convert_reduce_fusion
  542.5 2.0 copy.25
  544.5 3.3 copy.26
  547.8 3.2 fusion.2
  551.1 3.3 psum.45
  554.4 7.1 %psum.46 = f32[2304]{0:T(1024)S(1)} all-reduce(f32[2304]{0:T(1024)S(1)} %psum.45), channel_id=1, replica_groups=mesh['outer'=4,'mid'=2,'core'=2,'tensor'=2] {'mid'}, use_global_device_ids=true, to_apply=%region_8.0 | all-reduce | flops 2304 | bytes 18432 | tf_op jit(solution)/shard_map/psum | solution.py:63
  561.5 16.0 %psum.47 = f32[2304]{0:T(1024)S(1)} all-reduce(f32[2304]{0:T(1024)S(1)} %psum.46), channel_id=1, replica_groups=mesh['outer'=4,'mid'=2,'core'=2,'tensor'=2] {'outer'}, use_global_device_ids=true, to_apply=%region_9.0 | all-reduce | flops 2304 | bytes 18432 | tf_op jit(solution)/shard_map/psum | solution.py:63
  (41 shorter events, 6.1 us)
Async XLA Ops:
  7.2 149.8 %copy-start = (bf16[9216,16]{0,1:T(8,128)(2,1)S(1)}, bf16[9216,16]{0,1:T(8,128)(2,1)}, u32[]{:S(2)}) copy-start(bf16[9216,16]{0,1:T(8,128)(2,1)} %param.8) | copy-start | bytes 884740
  7.2 148.6 %copy-start.5 = (u32[32]{0:T(128)S(1)}, u32[32]{0:T(128)}, u32[]{:S(2)}) copy-start(u32[32]{0:T(128)} %constant.38) | copy-start | bytes 388
  7.2 149.8 %copy-start.3 = (bf16[16,288]{1,0:T(8,128)(2,1)S(1)}, bf16[16,288]{1,0:T(8,128)(2,1)}, u32[]{:S(2)}) copy-start(bf16[16,288]{1,0:T(8,128)(2,1)} %param.9) | copy-start | bytes 27652
  7.2 384.2 %all-gather.4.cloned.1.call-start = ((), (), s32[]{:S(2)}) async-start(), calls=%async_computation.2 | async-start | bytes 26542080 | tf_op jit(solution)/shard_map/all_gather | solution.py:22
  7.9 275.5 %collective-permute-start.1 = (bf16[320,9216]{1,0:T(8,128)(2,1)}, bf16[320,9216]{1,0:T(8,128)(2,1)}, u32[]{:S(2)}, u32[]{:S(2)}) collective-permute-start(bf16[320,9216]{1,0:T(8,128)(2,1)} %param.6), channel_id=1, source_target_pairs={{0,4},{4,0},{1,5},{5,1},{2,6},{6,2},{3,7},{7,3},{8,12},{12,8},{9,1... | collective-permute-start | bytes 17694728 | tf_op jit(solution)/shard_map/ppermute | solution.py:21
  11.0 311.8 %collective-permute-start = (bf16[320,9216]{1,0:T(8,128)(2,1)}, bf16[320,9216]{1,0:T(8,128)(2,1)}, u32[]{:S(2)}, u32[]{:S(2)}) collective-permute-start(bf16[320,9216]{1,0:T(8,128)(2,1)} %param.6), channel_id=1, source_target_pairs={{0,2},{2,0},{1,3},{3,1},{4,6},{6,4},{5,7},{7,5},{8,10},{10,8},{9,1... | collective-permute-start | bytes 17694728 | tf_op jit(solution)/shard_map/ppermute | solution.py:23
  157.0 90.0 %copy-start.4 = (f32[2304]{0:T(1024)S(1)}, f32[2304]{0:T(1024)}, u32[]{:S(2)}) copy-start(f32[2304]{0:T(1024)} %param.10) | copy-start | bytes 27652
  157.0 90.1 %copy-start.2 = (bf16[320,2304]{1,0:T(8,128)(2,1)S(1)}, bf16[320,2304]{1,0:T(8,128)(2,1)}, u32[]{:S(2)}) copy-start(bf16[320,2304]{1,0:T(8,128)(2,1)} %param.11) | copy-start | bytes 4423684
  266.6 54.8 %all-to-all-start = ((f32[16,16,720]{2,1,0:T(8,128)}), f32[16,16,720]{2,1,0:T(8,128)S(1)}, u32[]{:S(2)}, u32[]{:S(2)}) async-start(f32[16,16,720]{2,1,0:T(8,128)} %maximum_bitcast_fusion), calls=%async_computation | async-start | bytes 1572864 | tf_op jit(solution)/shard_map/all_to_all | solution.py:47
  283.4 9.2 %slice-start = ((s8[5898240]{0:T(1024)(128)(4,1)}), s8[1703936]{0:T(1024)(128)(4,1)S(1)}, s32[]{:S(2)}) async-start(s8[5898240]{0:T(1024)(128)(4,1)} %bitcast.41), calls=%async_computation.3 | async-start | bytes 3407872
  283.4 9.2 %slice-start.1 = ((s8[5898240]{0:T(1024)(128)(4,1)}), s8[4194304]{0:T(1024)(128)(4,1)S(1)}, s32[]{:S(2)}) async-start(s8[5898240]{0:T(1024)(128)(4,1)} %bitcast.41), calls=%async_computation.4 | async-start | bytes 8388608
  283.4 50.6 %collective-permute-start.2 = (bf16[320,9216]{1,0:T(8,128)(2,1)}, bf16[320,9216]{1,0:T(8,128)(2,1)}, u32[]{:S(2)}, u32[]{:S(2)}) collective-permute-start(bf16[320,9216]{1,0:T(8,128)(2,1)} %collective-permute-done.1), channel_id=1, source_target_pairs={{0,2},{2,0},{1,3},{3,1},{4,6},{6,4},{5,7},{7,5},{8,10},{10,8},{9,1... | collective-permute-start | bytes 17694728 | tf_op jit(solution)/shard_map/ppermute | solution.py:24
  492.8 46.6 %all-to-all-start.1 = ((bf16[8,2,320,288]{2,3,1,0:T(8,128)(2,1)}), bf16[8,2,320,288]{2,3,1,0:T(8,128)(2,1)}, u32[]{:S(2)}, u32[]{:S(2)}) async-start(bf16[8,2,320,288]{2,3,1,0:T(8,128)(2,1)} %bitcast.46), calls=%async_computation.1 | async-start | bytes 7077888 | tf_op jit(solution)/shard_map/all_to_all | solution.py:56
  544.5 33.6 %copy-start.1 = (bf16[9216,16]{0,1:T(8,128)(2,1)S(1)}, bf16[9216,16]{0,1:T(8,128)(2,1)}, u32[]{:S(2)}) copy-start(bf16[9216,16]{0,1:T(8,128)(2,1)} %param.8) | copy-start | bytes 884740
Sparse Core Ops, SparseCore 0:
  9.6 381.7 all-gather.3
